TPU v7x, 512 devices: a whole 4x8x8 slice. The times are simulated.
512 devices in a mesh: seq: 64 (over z_hi, x, y), head: 8 (over z_lo, core).
Axes of the slice: x: 4, y: 8, z: 8 (z_hi: 2, z_lo: 4; z = z_hi * 4 + z_lo), core: 2. Of those that a mesh axis runs over, the one named last changes fastest.
Arguments:
- queries: bfloat16 [12288, 32, 128], P('seq', 'head'), may hold values from -180 to 180
- key_rows: bfloat16 [12288, 8, 128], P('seq', 'head'), may hold values from -4.5 to 4.5
- value_rows: bfloat16 [12288, 8, 128], P('seq', 'head'), may hold values from -24 to 24
- windows: int32 [32], P('head'), may hold values from 768 to 1536, as said below
- sink_counts: int32 [32], P('head'), may hold values from 1 to 4, as said below
- sink_bias: float32 [32], P('head'), may hold values from 3 to 7
- out_weight: bfloat16 [4096, 4096], P('head'), may hold values from -0.09375 to 0.09375
Outputs:
- attn_out: bfloat16 [12288, 4096], P(('seq', 'head'))
Inputs may be any that keep to these rules, and one draw needn't show every extreme that they name: `windows`: each head's window lies between 768 and 1536, and some head has exactly 1536. `sink_counts`: each head has 1 to 4 sink tokens, and some head has exactly 4.
All inputs are finite; a program needn't handle non-finite values.
Results may differ from a plain program's by a relative error of at most 0.018.
Values may be sent and summed in bfloat16 or wider, within the bound.
A program may use at most 64 MiB of HBM per device.

v0:
```python
import jax
import jax.numpy as jnp
from jax import lax
from jax.sharding import Mesh
from jax.sharding import PartitionSpec as P

WINDOW = 1536
SINKS = 4
SEQ = ("seq_0", "seq_1", "seq_2")
SEQ_HEAD = ("seq_0", "seq_1", "seq_2", "head")


def shifted(block, axis, distance):
    devices = range(lax.axis_size(axis))
    route = [(i - distance, i) for i in devices if i - distance in devices]
    return lax.ppermute(block, axis, route)


def broadcast_by_axis(shard, axes, root):
    shard = jnp.where(lax.axis_index(axes) == root, shard, jnp.zeros_like(shard))
    for axis in axes:
        shard = lax.psum(shard, axis)
    return shard


def cut_along(shard, dim, length):
    dims = shard.shape
    blocks = shard.reshape(*dims[:dim], length, dims[dim] // length, *dims[dim + 1 :])
    return jnp.moveaxis(blocks, dim, 0)


def sent_and_summed(shard, axis, dim):
    blocks = cut_along(shard, dim, lax.axis_size(axis))
    arrived = lax.all_to_all(blocks, axis, split_axis=0, concat_axis=0, tiled=True)
    return arrived.astype(jnp.float32).sum(axis=0)


def attend_block(query_block, band_rows, sink_rows, first_pos, windows, sink_counts, sink_bias):
    tok_rows, local_heads, head_width = query_block.shape
    kv_local = band_rows.shape[2]
    group_size = local_heads // kv_local
    band_span = band_rows.shape[1]
    sink_total = sink_rows.shape[1]
    all_keys = jnp.concatenate([sink_rows[0], band_rows[0]], axis=0)
    all_values = jnp.concatenate([sink_rows[1], band_rows[1]], axis=0)
    grouped = query_block.reshape(tok_rows, kv_local, group_size, head_width)
    score_scale = 1.0 / head_width**0.5
    scores = (
        jnp.einsum("tkgd,skd->kgts", grouped, all_keys, preferred_element_type=jnp.float32)
        * score_scale
    )
    query_pos = first_pos + jnp.arange(tok_rows, dtype=jnp.int32)
    band_pos = first_pos + tok_rows - band_span + jnp.arange(band_span, dtype=jnp.int32)
    sink_pos = jnp.arange(sink_total, dtype=jnp.int32)
    key_pos = jnp.concatenate([sink_pos, band_pos])
    is_sink = jnp.concatenate([jnp.ones((sink_total,), bool), jnp.zeros((band_span,), bool)])
    head_window = windows.reshape(kv_local, group_size, 1, 1)
    head_sinks = sink_counts.reshape(kv_local, group_size, 1, 1)
    head_bias = sink_bias.reshape(kv_local, group_size, 1, 1)
    distance = query_pos[:, None] - key_pos[None, :]
    visible = (distance >= 0) & jnp.where(
        is_sink, key_pos < head_sinks, (distance < head_window) & (key_pos >= head_sinks)
    )
    scores = scores + jnp.where(is_sink, head_bias, 0.0)
    masked = jnp.where(visible, scores, -1e30)
    highest = jnp.max(masked, axis=-1, keepdims=True)
    weights = jnp.where(visible, jnp.exp(masked - highest), 0.0)
    normed = (weights / jnp.sum(weights, axis=-1, keepdims=True)).astype(jnp.bfloat16)
    mixed = jnp.einsum("kgts,skd->tkgd", normed, all_values, preferred_element_type=jnp.float32)
    return mixed.astype(jnp.bfloat16).reshape(tok_rows, local_heads * head_width)


def shards(queries, key_rows, value_rows, windows, sink_counts, sink_bias, out_weight):
    tok_rows = queries.shape[0]
    stacked = jnp.stack([key_rows, value_rows])
    halo_depth = (WINDOW - 1) // tok_rows + 1
    received = [shifted(stacked, SEQ, halo_depth - number) for number in range(halo_depth)]
    halo_rows = jnp.concatenate(received, axis=1)
    band_all = jnp.concatenate([halo_rows, stacked], axis=1)
    sink_rows = broadcast_by_axis(stacked[:, :SINKS], SEQ, 0)
    first_pos = lax.axis_index(SEQ) * tok_rows
    attended = attend_block(
        queries, band_all, sink_rows, first_pos, windows, sink_counts, sink_bias
    )
    mine = sent_and_summed(
        jnp.dot(attended, out_weight, preferred_element_type=jnp.float32).astype(jnp.bfloat16),
        "head",
        0,
    )
    return mine.astype(jnp.bfloat16)


def solution(mesh):
    split = Mesh(
        mesh.devices.reshape(2, 4, 8, mesh.shape["head"]), ("seq_0", "seq_1", "seq_2", "head")
    )
    return jax.shard_map(
        shards,
        mesh=split,
        in_specs=(
            P(SEQ, "head", None),
            P(SEQ, "head", None),
            P(SEQ, "head", None),
            P("head"),
            P("head"),
            P("head"),
            P("head", None),
        ),
        out_specs=P(SEQ_HEAD, None),
        check_vma=False,
    )
```

profile of v0, /device:TPU:256, one launch (start us, length us, event | category | flops | bytes accessed | tf_op | source)
XLA Modules:
  0.0 160.0 jit_solution(8025812477693680216)
XLA Ops:
  0.0 0.9 pad_maximum_fusion
  0.9 4.5 %collective-permute-start.6 = (bf16[2,192,1,128]{3,1,2,0:T(8,128)(2,1)S(1)}, bf16[2,192,1,128]{3,1,2,0:T(8,128)(2,1)S(1)}, u32[]{:S(2)}, u32[]{:S(2)}) collective-permute-start(bf16[2,192,1,128]{3,1,2,0:T(8,128)(2,1)S(1)} %pad_maximum_fusion), channel_id=1, source_target_pairs={{0,16},{8,24},{16,32},{24,40},{32,48},{40,56},{48,64},{56,72},{64,... | collective-permute-start | bytes 294920 | tf_op jit(solution)/shard_map/ppermute | solution.py:16
  5.4 5.8 %collective-permute-start.5 = (bf16[2,192,1,128]{3,1,2,0:T(8,128)(2,1)S(1)}, bf16[2,192,1,128]{3,1,2,0:T(8,128)(2,1)S(1)}, u32[]{:S(2)}, u32[]{:S(2)}) collective-permute-start(bf16[2,192,1,128]{3,1,2,0:T(8,128)(2,1)S(1)} %pad_maximum_fusion), channel_id=1, source_target_pairs={{0,24},{8,32},{16,40},{24,48},{32,56},{40,64},{48,72},{56,80},{64,... | collective-permute-start | bytes 294920 | tf_op jit(solution)/shard_map/ppermute | solution.py:16
  11.2 3.8 %collective-permute-start.4 = (bf16[2,192,1,128]{3,1,2,0:T(8,128)(2,1)S(1)}, bf16[2,192,1,128]{3,1,2,0:T(8,128)(2,1)S(1)}, u32[]{:S(2)}, u32[]{:S(2)}) collective-permute-start(bf16[2,192,1,128]{3,1,2,0:T(8,128)(2,1)S(1)} %pad_maximum_fusion), channel_id=1, source_target_pairs={{0,32},{8,40},{16,48},{24,56},{32,64},{40,72},{48,80},{56,88},{64,... | collective-permute-start | bytes 294920 | tf_op jit(solution)/shard_map/ppermute | solution.py:16
  15.1 6.0 %collective-permute-start.3 = (bf16[2,192,1,128]{3,1,2,0:T(8,128)(2,1)S(1)}, bf16[2,192,1,128]{3,1,2,0:T(8,128)(2,1)S(1)}, u32[]{:S(2)}, u32[]{:S(2)}) collective-permute-start(bf16[2,192,1,128]{3,1,2,0:T(8,128)(2,1)S(1)} %pad_maximum_fusion), channel_id=1, source_target_pairs={{0,40},{8,48},{16,56},{24,64},{32,72},{40,80},{48,88},{56,96},{64,... | collective-permute-start | bytes 294920 | tf_op jit(solution)/shard_map/ppermute | solution.py:16
  21.1 3.4 %collective-permute-start = (bf16[2,192,1,128]{3,1,2,0:T(8,128)(2,1)S(1)}, bf16[2,192,1,128]{3,1,2,0:T(8,128)(2,1)S(1)}, u32[]{:S(2)}, u32[]{:S(2)}) collective-permute-start(bf16[2,192,1,128]{3,1,2,0:T(8,128)(2,1)S(1)} %pad_maximum_fusion), channel_id=1, source_target_pairs={{0,64},{8,72},{16,80},{24,88},{32,96},{40,104},{48,112},{56,120},{... | collective-permute-start | bytes 294920 | tf_op jit(solution)/shard_map/ppermute | solution.py:16
  25.8 8.8 %psum.21 = bf16[2,4,1,128]{3,1,2,0:T(4,128)(2,1)S(1)} all-reduce(bf16[2,4,1,128]{3,1,2,0:T(4,128)(2,1)S(1)} %fusion.20), channel_id=1, replica_groups=mesh['seq_0'=2,'seq_1'=4,'seq_2'=8,'head'=8] {'seq_0'}, use_global_device_ids=true, to_apply=%region_0.1 | all-reduce | flops 1024 | bytes 4096 | tf_op jit(solution)/shard_map/psum | solution.py:22
  34.7 9.5 %psum.22 = bf16[2,4,1,128]{3,1,2,0:T(4,128)(2,1)S(1)} all-reduce(bf16[2,4,1,128]{3,1,2,0:T(4,128)(2,1)S(1)} %psum.21), channel_id=1, replica_groups=mesh['seq_0'=2,'seq_1'=4,'seq_2'=8,'head'=8] {'seq_1'}, use_global_device_ids=true, to_apply=%region_1.2 | all-reduce | flops 1024 | bytes 4096 | tf_op jit(solution)/shard_map/psum | solution.py:22
  44.1 16.7 %psum.23 = bf16[2,4,1,128]{3,1,2,0:T(4,128)(2,1)S(1)} all-reduce(bf16[2,4,1,128]{3,1,2,0:T(4,128)(2,1)S(1)} %psum.22), channel_id=1, replica_groups=mesh['seq_0'=2,'seq_1'=4,'seq_2'=8,'head'=8] {'seq_2'}, use_global_device_ids=true, to_apply=%region_2.3 | all-reduce | flops 1024 | bytes 4096 | tf_op jit(solution)/shard_map/psum | solution.py:22
  60.8 0.7 broadcast_compare_fusion.2
  61.6 0.8 broadcast_select_fusion
  62.4 3.9 %collective-permute-start.1 = (bf16[2,192,1,128]{3,1,2,0:T(8,128)(2,1)S(1)}, bf16[2,192,1,128]{3,1,2,0:T(8,128)(2,1)S(1)}, u32[]{:S(2)}, u32[]{:S(2)}) collective-permute-start(bf16[2,192,1,128]{3,1,2,0:T(8,128)(2,1)S(1)} %pad_maximum_fusion), channel_id=1, source_target_pairs={{0,56},{8,64},{16,72},{24,80},{32,88},{40,96},{48,104},{56,112},{6... | collective-permute-start | bytes 294920 | tf_op jit(solution)/shard_map/ppermute | solution.py:16
  66.3 9.5 %collective-permute-done.1 = bf16[2,192,1,128]{3,1,2,0:T(8,128)(2,1)S(1)} collective-permute-done((bf16[2,192,1,128]{3,1,2,0:T(8,128)(2,1)S(1)}, bf16[2,192,1,128]{3,1,2,0:T(8,128)(2,1)S(1)}, u32[]{:S(2)}, u32[]{:S(2)}) %collective-permute-start.1) | collective-permute-done | bytes 98336 | tf_op jit(solution)/shard_map/ppermute | solution.py:16
  75.8 3.3 %collective-permute-start.2 = (bf16[2,192,1,128]{3,1,2,0:T(8,128)(2,1)S(1)}, bf16[2,192,1,128]{3,1,2,0:T(8,128)(2,1)S(1)}, u32[]{:S(2)}, u32[]{:S(2)}) collective-permute-start(bf16[2,192,1,128]{3,1,2,0:T(8,128)(2,1)S(1)} %pad_maximum_fusion), channel_id=1, source_target_pairs={{0,48},{8,56},{16,64},{24,72},{32,80},{40,88},{48,96},{56,104},{64... | collective-permute-start | bytes 294920 | tf_op jit(solution)/shard_map/ppermute | solution.py:16
  79.2 10.9 %collective-permute-done.2 = bf16[2,192,1,128]{3,1,2,0:T(8,128)(2,1)S(1)} collective-permute-done((bf16[2,192,1,128]{3,1,2,0:T(8,128)(2,1)S(1)}, bf16[2,192,1,128]{3,1,2,0:T(8,128)(2,1)S(1)}, u32[]{:S(2)}, u32[]{:S(2)}) %collective-permute-start.2) | collective-permute-done | bytes 98336 | tf_op jit(solution)/shard_map/ppermute | solution.py:16
  90.1 5.0 %collective-permute-start.7 = (bf16[2,192,1,128]{3,1,2,0:T(8,128)(2,1)S(1)}, bf16[2,192,1,128]{3,1,2,0:T(8,128)(2,1)S(1)}, u32[]{:S(2)}, u32[]{:S(2)}) collective-permute-start(bf16[2,192,1,128]{3,1,2,0:T(8,128)(2,1)S(1)} %pad_maximum_fusion), channel_id=1, source_target_pairs={{0,8},{8,16},{16,24},{24,32},{32,40},{40,48},{48,56},{56,64},{64,7... | collective-permute-start | bytes 294920 | tf_op jit(solution)/shard_map/ppermute | solution.py:16
  95.2 9.5 %collective-permute-done.7 = bf16[2,192,1,128]{3,1,2,0:T(8,128)(2,1)S(1)} collective-permute-done((bf16[2,192,1,128]{3,1,2,0:T(8,128)(2,1)S(1)}, bf16[2,192,1,128]{3,1,2,0:T(8,128)(2,1)S(1)}, u32[]{:S(2)}, u32[]{:S(2)}) %collective-permute-start.7) | collective-permute-done | bytes 98336 | tf_op jit(solution)/shard_map/ppermute | solution.py:16
  104.7 0.8 constant_dynamic-update-slice_fusion
  105.7 2.3 %fusion.1 = (f32[4,192]{1,0:T(4,128)S(1)}, f32[1732,192,4]{0,1,2:T(8,128)S(1)}) fusion(f32[4,1732]{1,0:T(4,128)S(1)} %broadcast_select_fusion, s32[192,1732]{1,0:T(8,128)S(1)} %broadcast_subtract_fusion, s32[4]{0:T(128)S(1)} %copy-done.3, pred[4,1732]{1,0:T(4,128)(4,1)S(1)} %get-tuple-element.8, pred[4,1732]{1,0:T(4,128)(4,1)S(1)} %get-tuple-element.7, ...), kind=kOutput, calls=%fused_computation.6 | convolution fusion | flops 352052480 | bytes 7669812 | tf_op jit(solution)/shard_map/tkgd,skd->kgts/dot_general | solution.py:49
  108.0 3.5 %fusion.4 = f32[4,192]{1,0:T(4,128)S(1)} fusion(f32[4,192]{1,0:T(4,128)S(1)} %get-tuple-element.11, f32[4,1732]{1,0:T(4,128)S(1)} %broadcast_select_fusion, f32[1732,192,4]{0,1,2:T(8,128)S(1)} %get-tuple-element.12, pred[4,1732]{1,0:T(4,128)(4,1)S(1)} %get-tuple-element.8, s32[4]{0:T(128)S(1)} %copy-done.3, s32[192,1732]{1,0:T(8,128)S(1)} %broadcast_subtract_fusion, ...), kind=kLoop, calls=%fused_computation.9 | loop fusion | flops 13300992 | bytes 7032884 | tf_op jit(solution)/shard_map/reduce_sum | solution.py:68
  111.5 2.8 %fusion.8 = bf16[192,1,4,128]{3,0,2,1:T(8,128)(2,1)S(1)} fusion(f32[4,192]{1,0:T(4,128)S(1)} %fusion.4, f32[4,192]{1,0:T(4,128)S(1)} %get-tuple-element.11, f32[4,1732]{1,0:T(4,128)S(1)} %broadcast_select_fusion, f32[1732,192,4]{0,1,2:T(8,128)S(1)} %get-tuple-element.12, pred[4,1732]{1,0:T(4,128)(4,1)S(1)} %get-tuple-element.8, s32[4]{0:T(128)S(1)} %copy-done.3, ...), kind=kOutput, calls=%fused_computation.11 | convolution fusion | flops 356142080 | bytes 7672884 | tf_op jit(solution)/shard_map/kgts,skd->tkgd/dot_general | solution.py:69
  114.5 1.0 convolution_convert_fusion
  115.5 43.5 %all_to_all.5 = bf16[8,24,4096]{2,1,0:T(8,128)(2,1)S(1)} all-to-all(bf16[8,24,4096]{2,1,0:T(8,128)(2,1)S(1)} %bitcast.58), channel_id=1, replica_groups=mesh['seq_0'=2,'seq_1'=4,'seq_2'=8,'head'=8] {'head'}, dimensions={0} | all-to-all | bytes 3145728 | tf_op jit(solution)/shard_map/all_to_all | solution.py:34
  159.1 0.9 reduce_sum.22
  (31 shorter events, 1.6 us)
Async XLA Ops:
  0.0 105.7 %copy-start = (bf16[192,4,128]{2,1,0:T(4,128)(2,1)S(1)}, bf16[192,4,128]{2,1,0:T(4,128)(2,1)}, u32[]{:S(2)}) copy-start(bf16[192,4,128]{2,1,0:T(4,128)(2,1)} %param.7) | copy-start | bytes 589828
  0.0 105.7 %copy-start.2 = (pred[1732]{0:T(1024)(128)(4,1)S(1)}, pred[1732]{0:T(1024)(128)(4,1)}, u32[]{:S(2)}) copy-start(pred[1732]{0:T(1024)(128)(4,1)} %constant.37.clone.1) | copy-start | bytes 5200
  0.0 105.7 %copy-start.3 = (s32[4]{0:T(128)S(1)}, s32[4]{0:T(128)}, u32[]{:S(2)}) copy-start(s32[4]{0:T(128)} %param.10) | copy-start | bytes 52
  0.9 94.3 %collective-permute-start.6 = (bf16[2,192,1,128]{3,1,2,0:T(8,128)(2,1)S(1)}, bf16[2,192,1,128]{3,1,2,0:T(8,128)(2,1)S(1)}, u32[]{:S(2)}, u32[]{:S(2)}) collective-permute-start(bf16[2,192,1,128]{3,1,2,0:T(8,128)(2,1)S(1)} %pad_maximum_fusion), channel_id=1, source_target_pairs={{0,16},{8,24},{16,32},{24,40},{32,48},{40,56},{48,64},{56,72},{64,... | collective-permute-start | bytes 294920 | tf_op jit(solution)/shard_map/ppermute | solution.py:16
  5.4 89.8 %collective-permute-start.5 = (bf16[2,192,1,128]{3,1,2,0:T(8,128)(2,1)S(1)}, bf16[2,192,1,128]{3,1,2,0:T(8,128)(2,1)S(1)}, u32[]{:S(2)}, u32[]{:S(2)}) collective-permute-start(bf16[2,192,1,128]{3,1,2,0:T(8,128)(2,1)S(1)} %pad_maximum_fusion), channel_id=1, source_target_pairs={{0,24},{8,32},{16,40},{24,48},{32,56},{40,64},{48,72},{56,80},{64,... | collective-permute-start | bytes 294920 | tf_op jit(solution)/shard_map/ppermute | solution.py:16
  11.2 83.9 %collective-permute-start.4 = (bf16[2,192,1,128]{3,1,2,0:T(8,128)(2,1)S(1)}, bf16[2,192,1,128]{3,1,2,0:T(8,128)(2,1)S(1)}, u32[]{:S(2)}, u32[]{:S(2)}) collective-permute-start(bf16[2,192,1,128]{3,1,2,0:T(8,128)(2,1)S(1)} %pad_maximum_fusion), channel_id=1, source_target_pairs={{0,32},{8,40},{16,48},{24,56},{32,64},{40,72},{48,80},{56,88},{64,... | collective-permute-start | bytes 294920 | tf_op jit(solution)/shard_map/ppermute | solution.py:16
  15.1 80.0 %collective-permute-start.3 = (bf16[2,192,1,128]{3,1,2,0:T(8,128)(2,1)S(1)}, bf16[2,192,1,128]{3,1,2,0:T(8,128)(2,1)S(1)}, u32[]{:S(2)}, u32[]{:S(2)}) collective-permute-start(bf16[2,192,1,128]{3,1,2,0:T(8,128)(2,1)S(1)} %pad_maximum_fusion), channel_id=1, source_target_pairs={{0,40},{8,48},{16,56},{24,64},{32,72},{40,80},{48,88},{56,96},{64,... | collective-permute-start | bytes 294920 | tf_op jit(solution)/shard_map/ppermute | solution.py:16
  21.1 41.2 %collective-permute-start = (bf16[2,192,1,128]{3,1,2,0:T(8,128)(2,1)S(1)}, bf16[2,192,1,128]{3,1,2,0:T(8,128)(2,1)S(1)}, u32[]{:S(2)}, u32[]{:S(2)}) collective-permute-start(bf16[2,192,1,128]{3,1,2,0:T(8,128)(2,1)S(1)} %pad_maximum_fusion), channel_id=1, source_target_pairs={{0,64},{8,72},{16,80},{24,88},{32,96},{40,104},{48,112},{56,120},{... | collective-permute-start | bytes 294920 | tf_op jit(solution)/shard_map/ppermute | solution.py:16
  62.4 13.4 %collective-permute-start.1 = (bf16[2,192,1,128]{3,1,2,0:T(8,128)(2,1)S(1)}, bf16[2,192,1,128]{3,1,2,0:T(8,128)(2,1)S(1)}, u32[]{:S(2)}, u32[]{:S(2)}) collective-permute-start(bf16[2,192,1,128]{3,1,2,0:T(8,128)(2,1)S(1)} %pad_maximum_fusion), channel_id=1, source_target_pairs={{0,56},{8,64},{16,72},{24,80},{32,88},{40,96},{48,104},{56,112},{6... | collective-permute-start | bytes 294920 | tf_op jit(solution)/shard_map/ppermute | solution.py:16
  75.8 14.3 %collective-permute-start.2 = (bf16[2,192,1,128]{3,1,2,0:T(8,128)(2,1)S(1)}, bf16[2,192,1,128]{3,1,2,0:T(8,128)(2,1)S(1)}, u32[]{:S(2)}, u32[]{:S(2)}) collective-permute-start(bf16[2,192,1,128]{3,1,2,0:T(8,128)(2,1)S(1)} %pad_maximum_fusion), channel_id=1, source_target_pairs={{0,48},{8,56},{16,64},{24,72},{32,80},{40,88},{48,96},{56,104},{64... | collective-permute-start | bytes 294920 | tf_op jit(solution)/shard_map/ppermute | solution.py:16
  90.1 14.6 %collective-permute-start.7 = (bf16[2,192,1,128]{3,1,2,0:T(8,128)(2,1)S(1)}, bf16[2,192,1,128]{3,1,2,0:T(8,128)(2,1)S(1)}, u32[]{:S(2)}, u32[]{:S(2)}) collective-permute-start(bf16[2,192,1,128]{3,1,2,0:T(8,128)(2,1)S(1)} %pad_maximum_fusion), channel_id=1, source_target_pairs={{0,8},{8,16},{16,24},{24,32},{32,40},{40,48},{48,56},{56,64},{64,7... | collective-permute-start | bytes 294920 | tf_op jit(solution)/shard_map/ppermute | solution.py:16
  111.5 3.0 %copy-start.1 = (bf16[512,4096]{1,0:T(8,128)(2,1)S(1)}, bf16[512,4096]{1,0:T(8,128)(2,1)}, u32[]{:S(2)}) copy-start(bf16[512,4096]{1,0:T(8,128)(2,1)} %param.13) | copy-start | bytes 12582916
where the time goes:
time: 161 us; the launch traced here: 160 us
  blocking collectives  78.5 us (49%)
  starting transfers between devices  35.8 us (22%)
  waiting for transfers between devices  29.9 us (19%)
  other arithmetic  8.87 us (6%)
  matrix products  6.17 us (4%)
    all_to_all x1, blocking collectives, sent_and_summed(): lax.all_to_all(blocks, axis, split_axis=0, concat_axis=0, tiled=True)  43.5 us
    ppermute x8, starting transfers between devices, shifted(): return lax.ppermute(block, axis, route)  35.8 us
    psum x3, blocking collectives, broadcast_by_axis(): shard = lax.psum(shard, axis)  35 us
    ppermute x8, waiting for transfers between devices, shifted(): return lax.ppermute(block, axis, route)  29.9 us
    reduce_sum x1, other arithmetic, attend_block(): jnp.sum(weights, axis=-1, keepdims=True)  3.48 us
  transfers between devices with their start and end apart: 8, of which 3 were waited for; matrix products, arithmetic and copies ran while one was open for 2% of the time, Pallas kernels for 0%

commit v1 on v0

v1 whole, which is shorter than its diff:
```python
import jax
import jax.numpy as jnp
from jax import lax
from jax.experimental import pallas as pl
from jax.experimental.pallas import tpu as pltpu
from jax.sharding import PartitionSpec as P

TOK = 192
HEADS = 4
HD = 128
ROWS = TOK * HEADS
HALF = ROWS // 2
OUT_TOK = 24
D = 4096
NC = 4
CN = D // NC
KW = HEADS * HD
SINK_PAD = 16
LANES = 256
NEG = -1e30
LOG2E = 1.4426950408889634
MESH = pl.DeviceIdType.MESH
BF = jnp.bfloat16
F32 = jnp.float32


def remote(src, dst, send, recv, seq, head):
    return pltpu.make_async_remote_copy(
        src_ref=src, dst_ref=dst, send_sem=send, recv_sem=recv,
        device_id=(seq, head), device_id_type=MESH,
    )


def kernel(win_ref, cnt_ref, bias_ref, q_ref, k_ref, v_ref, w_ref, o_ref,
           kv, sink, q_in, q_f, q_f2, qs, w_own, w_oth, acc, m_st, l_st, a_buf, a_oth, pacc,
           sbuf, rbuf, relay,
           in_sem, x_send, y_send, kv_recv, s_send, s_recv, w_send, w_recv, a_send, a_recv,
           z_send, z_recv, relay_recv):
    seq = lax.axis_index("seq")
    head = lax.axis_index("head")
    row, y = seq // 8, seq % 8
    zl, core = head // 2, head % 2
    partner = head + 1 - 2 * core

    kv_in = [
        pltpu.make_async_copy(k_ref, kv.at[0, 0], in_sem.at[0]),
        pltpu.make_async_copy(v_ref, kv.at[0, 1], in_sem.at[1]),
    ]
    q_copy = pltpu.make_async_copy(q_ref, q_in, in_sem.at[2])
    w_copy = pltpu.make_async_copy(w_ref, w_own, in_sem.at[3])
    for copy in kv_in:
        copy.start()
    q_copy.start()
    w_copy.start()

    barrier = pltpu.get_barrier_semaphore()

    def greet(s, h):
        pl.semaphore_signal(barrier, inc=1, device_id=(s, h), device_id_type=MESH)

    @pl.when(row < 7)
    def _():
        greet(seq + 8, head)

    @pl.when(row > 0)
    def _():
        greet(seq - 8, head)

    for d in range(1, 8):
        greet(row * 8 + (y + d) % 8, head)
    greet(seq, partner)
    for d in range(1, 4):
        greet(seq, ((zl + d) % 4) * 2 + core)

    first = (row == 0) & (y == 0)
    later_first = (row > 0) & (y == 0)

    @pl.when(first)
    def _():
        for r in range(1, 8):
            greet(r * 8, head)

    @pl.when(later_first)
    def _():
        greet(0, head)

    expect = 11 + jnp.where(row < 7, 1, 0) + jnp.where(row > 0, 1, 0)
    expect = expect + jnp.where(first, 7, 0) + jnp.where(later_first, 1, 0)
    pl.semaphore_wait(barrier, expect)

    for copy in kv_in:
        copy.wait()

    def x_hop(part):
        return remote(kv.at[0, part], kv.at[8, part], x_send.at[part], kv_recv.at[8, part], seq + 8, head)

    def y_hop(source, d, part):
        return remote(kv.at[source, part], kv.at[d, part], y_send.at[d, part], kv_recv.at[d, part],
                      row * 8 + (y + d) % 8, head)

    order = (4, 3, 5, 2, 6, 1, 7)

    @pl.when(row < 7)
    def _():
        for part in range(2):
            x_hop(part).start()

    for d in order:
        @pl.when(y + d < 8)
        def _(d=d):
            for part in range(2):
                y_hop(0, d, part).start()

    sink_src = kv.at[0, :, pl.ds(0, SINK_PAD), :]

    def sink_row(r):
        return remote(sink_src, sink, s_send.at[r], s_recv, r * 8, head)

    def sink_y(src, d):
        return remote(src, sink, s_send.at[7 + d], s_recv, row * 8 + d, head)

    @pl.when(first)
    def _():
        for r in range(1, 8):
            sink_row(r).start()
        for d in range(1, 8):
            sink_y(sink_src, d).start()

    w_hop = remote(w_ref, w_oth, w_send, w_recv, seq, partner)
    w_hop.start()

    q_copy.wait()
    q_f[...] = q_in[...].astype(F32)
    for p in range(2):
        for h in range(HEADS):
            for d in range(4):
                q_f2[pl.ds(p * HALF + h * 96 + d * OUT_TOK, OUT_TOK), :] = q_f[
                    pl.ds((2 * d + p) * OUT_TOK * HEADS + h, OUT_TOK, HEADS), :]
    qs[...] = q_f2[...].astype(BF)

    m_st[...] = jnp.full_like(m_st, NEG)
    l_st[...] = jnp.zeros_like(l_st)
    acc[...] = jnp.zeros_like(acc)
    scale2 = LOG2E / HD ** 0.5

    def column_facts(tile):
        col = tile * LANES + lax.broadcasted_iota(jnp.int32, (1, LANES), 1)
        p = col // HALF
        h = (col % HALF) // 96
        token = (2 * ((col % 96) // OUT_TOK) + p) * OUT_TOK + col % OUT_TOK

        def per_head(ref):
            value = jnp.where(h == 0, ref[0], ref[1])
            value = jnp.where(h == 2, ref[2], value)
            return jnp.where(h == 3, ref[3], value)

        return seq * TOK + token, per_head

    def fold(tile, scores, values):
        lanes = pl.ds(tile * LANES, LANES)
        m_old = m_st[:, lanes]
        m_new = jnp.maximum(m_old, jnp.max(scores, axis=0, keepdims=True))
        weights = jnp.exp2(scores - m_new)
        alpha = jnp.exp2(m_old - m_new)
        m_st[:, lanes] = m_new
        l_st[:, lanes] = l_st[:, lanes] * alpha + jnp.sum(weights, axis=0, keepdims=True)
        mixed = lax.dot_general(values, weights.astype(BF), (((0,), (0,)), ((), ())),
                                preferred_element_type=F32)
        acc[:, lanes] = acc[:, lanes] * alpha + mixed

    def score_tile(tile, keys):
        return lax.dot_general(keys, qs[pl.ds(tile * LANES, LANES), :], (((1,), (1,)), ((), ())),
                               preferred_element_type=F32) * scale2

    def attend(slot):
        keys, values = kv[slot, 0], kv[slot, 1]
        for tile in range(ROWS // LANES):
            pos, per_head = column_facts(tile)
            key_pos = (seq - slot) * TOK + lax.broadcasted_iota(jnp.int32, (TOK, LANES), 0)
            distance = pos - key_pos
            visible = (distance >= 0) & (distance < per_head(win_ref)) & (key_pos >= per_head(cnt_ref))
            fold(tile, jnp.where(visible, score_tile(tile, keys), NEG), values)

    def attend_sinks():
        keys, values = sink[0], sink[1]
        for tile in range(ROWS // LANES):
            pos, per_head = column_facts(tile)
            key_pos = lax.broadcasted_iota(jnp.int32, (SINK_PAD, LANES), 0)
            visible = (pos >= key_pos) & (key_pos < per_head(cnt_ref))
            scores = score_tile(tile, keys) + per_head(bias_ref) * LOG2E
            fold(tile, jnp.where(visible, scores, NEG), values)

    @pl.when(first)
    def _():
        sink[...] = kv[0, :, :SINK_PAD, :]

    def sink_arrival():
        return remote(sink, sink, s_send.at[0], s_recv, seq, partner)

    def kv_arrival(slot, part):
        return remote(kv.at[slot, part], kv.at[slot, part], y_send.at[0, part], kv_recv.at[slot, part], seq, partner)

    @pl.when(row > 0)
    def _():
        for part in range(2):
            kv_arrival(8, part).wait_recv()
            for d in order:
                @pl.when(y + d >= 8)
                def _(d=d, part=part):
                    y_hop(8, d, part).start()

    @pl.when(jnp.logical_not(first))
    def _():
        sink_arrival().wait_recv()

    @pl.when(later_first)
    def _():
        for d in range(1, 8):
            sink_y(sink, d).start()

    def step(slot, carry):
        @pl.when(seq >= slot)
        def _():
            @pl.when((slot > 0) & (slot < 8))
            def _():
                for part in range(2):
                    kv_arrival(slot, part).wait_recv()

            attend(slot)

        return carry

    lax.fori_loop(0, 9, step, 0)
    attend_sinks()

    for tile in range(ROWS // 128):
        lanes = pl.ds(tile * 128, 128)
        done = acc[:, lanes] / l_st[:, lanes]
        a_buf[lanes, :] = done.T.astype(BF)

    mine = pl.multiple_of(core * HALF, HALF)
    theirs = pl.multiple_of(HALF - core * HALF, HALF)
    a_hop = remote(a_buf.at[pl.ds(theirs, HALF), :], a_oth, a_send, a_recv, seq, partner)
    a_hop.start()

    a_mine = jnp.concatenate(
        [a_buf[pl.ds(pl.multiple_of(mine + h * 96, 96), 96), :] for h in range(HEADS)], axis=1)
    w_copy.wait()

    for j in range(NC):
        cols = pl.ds(j * CN, CN)
        pacc[:, cols] = jnp.dot(a_mine, w_own[:, cols], preferred_element_type=F32)
    a_hop.wait_recv()
    w_hop.wait_recv()
    a_other = jnp.concatenate([a_oth[pl.ds(h * 96, 96), :] for h in range(HEADS)], axis=1)

    is_end = (zl == 0) | (zl == 3)
    is_mid = jnp.logical_not(is_end)
    n1 = 1 + zl // 3
    n2 = 3 - n1
    n3 = 3 - zl
    e1 = (zl - 1) * 3
    m2 = 3 - zl
    e2 = 3 - e1

    def item(d, j):
        return pacc[pl.ds(pl.multiple_of(d * OUT_TOK, 8), OUT_TOK), pl.ds(j * CN, CN)]

    def z_hop(n, j, to):
        return remote(sbuf.at[n, j], rbuf.at[zl, j], z_send.at[n, j], z_recv.at[zl, j], seq, to * 2 + core)

    def relay_hop(j):
        return remote(sbuf.at[2, j], relay.at[j], z_send.at[2, j], relay_recv.at[j], seq, n1 * 2 + core)

    def relay_arrival(j):
        return remote(relay.at[j], relay.at[j], z_send.at[2, j], relay_recv.at[j], seq, partner)

    def z_arrival(source, j):
        return remote(rbuf.at[source, j], rbuf.at[source, j], z_send.at[0, j], z_recv.at[source, j], seq, partner)

    for j in range(NC):
        cols = pl.ds(j * CN, CN)
        pacc[:, cols] += jnp.dot(a_other, w_oth[:, cols], preferred_element_type=F32)

        @pl.when(is_end)
        def _(j=j):
            sbuf[2, j] = item(n3, j).astype(BF)
            relay_hop(j).start()

        @pl.when(is_mid)
        def _(j=j):
            sbuf[0, j] = item(m2, j).astype(BF)
            z_hop(0, j, m2).start()
            sbuf[1, j] = item(e1, j).astype(BF)
            z_hop(1, j, e1).start()

    @pl.when(is_end)
    def _():
        for n, to in ((0, n2), (1, n1)):
            for j in range(NC):
                sbuf[n, j] = item(to, j).astype(BF)
                z_hop(n, j, to).start()

    @pl.when(is_mid)
    def _():
        for j in range(NC):
            relay_arrival(j).wait_recv()
            sbuf[2, j] = (item(e2, j) + relay[j].astype(F32)).astype(BF)
            z_hop(2, j, e2).start()

    def collect(sources):
        for j in range(NC):
            total = item(zl, j)
            for source in sources:
                z_arrival(source, j).wait_recv()
                total = total + rbuf[source, j].astype(F32)
            o_ref[:, pl.ds(j * CN, CN)] = total.astype(BF)

    @pl.when(is_end)
    def _():
        collect((n1, n2))

    @pl.when(is_mid)
    def _():
        collect((m2, e1, e2))

    @pl.when(row < 7)
    def _():
        for part in range(2):
            x_hop(part).wait_send()

    for d in order:
        @pl.when((y + d < 8) | (row > 0))
        def _(d=d):
            for part in range(2):
                y_hop(0, d, part).wait_send()

    @pl.when(first)
    def _():
        for r in range(1, 8):
            sink_row(r).wait_send()

    @pl.when(y == 0)
    def _():
        for d in range(1, 8):
            sink_y(sink, d).wait_send()

    w_hop.wait_send()
    a_hop.wait_send()
    for j in range(NC):
        for n in range(3):
            z_hop(n, j, zl).wait_send()


def shards(queries, key_rows, value_rows, windows, sink_counts, sink_bias, out_weight):
    smem = pl.BlockSpec(memory_space=pltpu.SMEM)
    hbm = pl.BlockSpec(memory_space=pl.ANY)
    return pl.pallas_call(
        kernel,
        out_shape=jax.ShapeDtypeStruct((OUT_TOK, D), BF),
        in_specs=[smem] * 3 + [hbm] * 4,
        out_specs=pl.BlockSpec(memory_space=pltpu.VMEM),
        scratch_shapes=[
            pltpu.VMEM((9, 2, TOK, HD), BF),
            pltpu.VMEM((2, SINK_PAD, HD), BF),
            pltpu.VMEM((ROWS, HD), BF),
            pltpu.VMEM((ROWS, HD), F32),
            pltpu.VMEM((ROWS, HD), F32),
            pltpu.VMEM((ROWS, HD), BF),
            pltpu.VMEM((KW, D), BF),
            pltpu.VMEM((KW, D), BF),
            pltpu.VMEM((HD, ROWS), F32),
            pltpu.VMEM((1, ROWS), F32),
            pltpu.VMEM((1, ROWS), F32),
            pltpu.VMEM((ROWS, HD), BF),
            pltpu.VMEM((HALF, HD), BF),
            pltpu.VMEM((96, D), F32),
            pltpu.VMEM((3, NC, OUT_TOK, CN), BF),
            pltpu.VMEM((4, NC, OUT_TOK, CN), BF),
            pltpu.VMEM((NC, OUT_TOK, CN), BF),
            pltpu.SemaphoreType.DMA((4,)),
            pltpu.SemaphoreType.DMA((2,)),
            pltpu.SemaphoreType.DMA((8, 2)),
            pltpu.SemaphoreType.DMA((9, 2)),
            pltpu.SemaphoreType.DMA((15,)),
            pltpu.SemaphoreType.DMA,
            pltpu.SemaphoreType.DMA,
            pltpu.SemaphoreType.DMA,
            pltpu.SemaphoreType.DMA,
            pltpu.SemaphoreType.DMA,
            pltpu.SemaphoreType.DMA((3, NC)),
            pltpu.SemaphoreType.DMA((4, NC)),
            pltpu.SemaphoreType.DMA((NC,)),
        ],
        compiler_params=pltpu.CompilerParams(
            collective_id=0, has_side_effects=True, vmem_limit_bytes=40 * 1024 * 1024),
    )(windows, sink_counts, sink_bias, queries.reshape(ROWS, HD), key_rows.reshape(TOK, HD),
      value_rows.reshape(TOK, HD), out_weight)


def solution(mesh):
    return jax.shard_map(
        shards,
        mesh=mesh,
        in_specs=(
            P("seq", "head", None),
            P("seq", "head", None),
            P("seq", "head", None),
            P("head"),
            P("head"),
            P("head"),
            P("head", None),
        ),
        out_specs=P(("seq", "head"), None),
        check_vma=False,
    )
```

time: 161 us -> 67.6 us (0.42)
  the two profiles are of different devices: /device:TPU:256 before, /device:TPU:257 now
where the time goes in v1:
time: 67.6 us; the launch traced here: 67.3 us
  Pallas kernels  59.9 us (89%)
  local copies, waits for them, and re-layouts  7.35 us (11%)
    pallas_call x1, Pallas kernels, shards(): pl.pallas_call(kernel, out_shape=jax.ShapeDtypeStruct((OUT_TOK, D), BF),...  59.9 us
    unnamed x15, local copies, waits for them, and re-layouts  7.35 us

profile of v1, /device:TPU:257, one launch (start us, length us, event | category | flops | bytes accessed | tf_op | source)
XLA Modules:
  0.0 67.3 jit_solution(14189070433617409983)
XLA Ops:
  0.0 0.0 copy-start
  0.0 2.2 %copy-done = bf16[512,4096]{1,0:T(8,128)(2,1)S(1)} copy-done((bf16[512,4096]{1,0:T(8,128)(2,1)S(1)}, bf16[512,4096]{1,0:T(8,128)(2,1)}, u32[]{:S(2)}) %copy-start) | copy-done | bytes 4194328
  2.2 0.0 copy-start.1
  2.2 0.9 %copy-done.1 = bf16[192,4,128]{2,1,0:T(4,128)(2,1)S(1)} copy-done((bf16[192,4,128]{2,1,0:T(4,128)(2,1)S(1)}, bf16[192,4,128]{2,1,0:T(4,128)(2,1)}, u32[]{:S(2)}) %copy-start.1) | copy-done | bytes 196632
  3.1 0.0 copy-start.2
  3.1 0.8 %copy-done.2 = bf16[192,1,128]{2,0,1:T(8,128)(2,1)S(1)} copy-done((bf16[192,1,128]{2,0,1:T(8,128)(2,1)S(1)}, bf16[192,1,128]{2,0,1:T(8,128)(2,1)}, u32[]{:S(2)}) %copy-start.2) | copy-done | bytes 49176
  3.9 0.0 copy-start.3
  3.9 0.8 %copy-done.3 = bf16[192,1,128]{2,0,1:T(8,128)(2,1)S(1)} copy-done((bf16[192,1,128]{2,0,1:T(8,128)(2,1)S(1)}, bf16[192,1,128]{2,0,1:T(8,128)(2,1)}, u32[]{:S(2)}) %copy-start.3) | copy-done | bytes 49176
  4.7 0.0 copy-start.4
  4.7 0.7 copy-done.4
  5.4 0.0 copy-start.5
  5.4 0.7 copy-done.5
  6.0 0.0 copy-start.6
  6.0 0.7 copy-done.6
  6.7 59.9 %shard_map.73 = bf16[24,4096]{1,0:T(8,128)(2,1)S(1)} custom-call(s32[4]{0:T(128)S(1)} %copy-done.4, s32[4]{0:T(128)S(1)} %copy-done.5, f32[4]{0:T(128)S(1)} %copy-done.6, bf16[768,128]{1,0:T(8,128)(2,1)S(1)} %bitcast.3, bf16[192,128]{1,0:T(8,128)(2,1)S(1)} %bitcast.4, bf16[192,128]{1,0:T(8,128)(2,1)S(1)} %bitcast.5, bf16[512,4096]{1,0:T(8,128)(2,1)S(1)} %copy-done), custom_call_target="tpu_custom_call" | custom-call | tf_op jit(solution)/shard_map/pallas_call | solution.py:358
  66.6 0.7 %copy.9 = bf16[24,4096]{1,0:T(8,128)(2,1)} copy(bf16[24,4096]{1,0:T(8,128)(2,1)S(1)} %shard_map.73) | data formatting | bytes 393216
Async XLA Ops:
  0.0 2.2 %copy-start = (bf16[512,4096]{1,0:T(8,128)(2,1)S(1)}, bf16[512,4096]{1,0:T(8,128)(2,1)}, u32[]{:S(2)}) copy-start(bf16[512,4096]{1,0:T(8,128)(2,1)} %w_ref.1) | copy-start | bytes 12582916
  2.2 0.9 %copy-start.1 = (bf16[192,4,128]{2,1,0:T(4,128)(2,1)S(1)}, bf16[192,4,128]{2,1,0:T(4,128)(2,1)}, u32[]{:S(2)}) copy-start(bf16[192,4,128]{2,1,0:T(4,128)(2,1)} %param.7) | copy-start | bytes 589828
  3.1 0.8 %copy-start.2 = (bf16[192,1,128]{2,0,1:T(8,128)(2,1)S(1)}, bf16[192,1,128]{2,0,1:T(8,128)(2,1)}, u32[]{:S(2)}) copy-start(bf16[192,1,128]{2,0,1:T(8,128)(2,1)} %param.8) | copy-start | bytes 147460
  3.9 0.8 %copy-start.3 = (bf16[192,1,128]{2,0,1:T(8,128)(2,1)S(1)}, bf16[192,1,128]{2,0,1:T(8,128)(2,1)}, u32[]{:S(2)}) copy-start(bf16[192,1,128]{2,0,1:T(8,128)(2,1)} %param.9) | copy-start | bytes 147460
  4.7 0.7 copy-start.4
  5.4 0.7 copy-start.5
  6.0 0.7 copy-start.6

commit v2 on v1

v2 whole, which is shorter than its diff:
```python
import jax
import jax.numpy as jnp
from jax import lax
from jax.experimental import pallas as pl
from jax.experimental.pallas import tpu as pltpu
from jax.sharding import PartitionSpec as P

TOK = 192
HEADS = 4
HD = 128
ROWS = TOK * HEADS
HALF = ROWS // 2
OUT_TOK = 24
D = 4096
NC = 4
CN = D // NC
KW = HEADS * HD
SINK_PAD = 16
PARTS = 4
PART_ROWS = 2 * TOK // PARTS
LANES = 256
NEG = -1e30
LOG2E = 1.4426950408889634
MESH = pl.DeviceIdType.MESH
BF = jnp.bfloat16
F32 = jnp.float32


USUAL = (
    (8, 1, 2, 7, 6, 5, 3, 4),
    (1, 8, 7, 6, 2, 5, 3, 4),
    (1, 8, 2, 7, 6, 5, 3, 4),
    (1, 8, 2, 7, 3, 6, 5, 4),
    (1, 8, 2, 7, 3, 6, 5, 4),
    (1, 8, 7, 2, 6, 3, 5, 4),
    (8, 7, 2, 6, 1, 5, 3, 4),
    (8, 7, 6, 1, 3, 5, 2, 4),
)
CROSSED = (
    (8, 1, 7, 2, 6, 5, 3, 4),
    (1, 8, 7, 6, 2, 5, 3, 4),
    (1, 2, 8, 7, 6, 5, 3, 4),
    (1, 2, 8, 3, 7, 6, 5, 4),
    (1, 2, 8, 7, 3, 6, 4, 5),
    (1, 2, 8, 7, 3, 6, 4, 5),
    (1, 2, 8, 7, 3, 6, 5, 4),
    (1, 7, 8, 3, 6, 5, 2, 4),
)
TOP = (
    (8, 1, 2, 3, 4, 5, 6, 7),
    (8, 1, 2, 3, 4, 5, 6, 7),
    (8, 1, 2, 3, 4, 5, 6, 7),
    (8, 1, 2, 3, 4, 5, 6, 7),
    (8, 1, 2, 3, 4, 5, 6, 7),
    (8, 1, 2, 3, 5, 4, 6, 7),
    (8, 1, 2, 6, 3, 5, 4, 7),
    (8, 7, 1, 6, 3, 5, 2, 4),
)


def packed(order):
    return sum((slot - 1) << (3 * k) for k, slot in enumerate(order))


def remote(src, dst, send, recv, seq, head):
    return pltpu.make_async_remote_copy(
        src_ref=src, dst_ref=dst, send_sem=send, recv_sem=recv,
        device_id=(seq, head), device_id_type=MESH,
    )


def kernel(win_in, cnt_in, bias_in, q_ref, k_ref, v_ref, w_ref, o_ref,
           win_ref, cnt_ref, bias_ref, kv, sink, q_in, q_f, q_f2, qs, w_own, w_oth, acc, m_st, l_st, a_buf, a_oth, pacc,
           sbuf, rbuf, relay,
           in_sem, x_send, y_send, far_send, kv_recv, s_send, s_recv, w_send, w_recv, a_send, a_recv,
           z_send, z_recv, relay_recv):
    seq = lax.axis_index("seq")
    head = lax.axis_index("head")
    row, y = seq // 8, seq % 8
    zl, core = head // 2, head % 2
    partner = head + 1 - 2 * core

    half = TOK // PART_ROWS
    kv_in = [
        pltpu.make_async_copy(
            ref.at[pl.ds(i * PART_ROWS, PART_ROWS), :], kv.at[0, base + i], in_sem.at[base + i])
        for base, ref in ((0, k_ref), (half, v_ref))
        for i in range(half)
    ]
    later_in = [
        pltpu.make_async_copy(q_ref, q_in, in_sem.at[PARTS]),
        pltpu.make_async_copy(win_in, win_ref, in_sem.at[PARTS + 2]),
        pltpu.make_async_copy(cnt_in, cnt_ref, in_sem.at[PARTS + 3]),
        pltpu.make_async_copy(bias_in, bias_ref, in_sem.at[PARTS + 4]),
    ]
    w_copy = pltpu.make_async_copy(w_ref, w_own, in_sem.at[PARTS + 1])
    for copy in kv_in + later_in:
        copy.start()
    w_copy.start()

    is_end = (zl == 0) | (zl == 3)
    is_mid = jnp.logical_not(is_end)
    n1 = 1 + zl // 3
    n2 = 3 - n1
    n3 = 3 - zl
    e1 = (zl - 1) * 3
    m2 = 3 - zl
    e2 = 3 - e1
    first = (row == 0) & (y == 0)
    inner = row > 0

    barrier = pltpu.get_barrier_semaphore()

    def greet(s, h, when=None):
        def signal():
            pl.semaphore_signal(barrier, inc=1, device_id=(s, h), device_id_type=MESH)

        if when is None:
            signal()
        else:
            pl.when(when)(signal)

    greet(seq - 1, head, y >= 1)
    greet(seq + 1, head, (y <= 6) & (inner | (y >= 5)))
    for d in (5, 6, 7):
        greet(seq + d, head, (y == 0) & inner)
    for d in (7, 6, 5):
        greet(seq - d, head, y == 7)
    greet(jnp.where(row == 0, seq + 24, jnp.where(row == 4, seq - 32, seq - 8)), head)
    greet(seq - 24, head, (row == 3) | (row == 7))
    greet(row * 8, head, (row == 0) & (y >= 1))
    greet(seq, partner)
    greet(seq, n1 * 2 + core, is_end)
    greet(seq, n2 * 2 + core, is_end)
    for d in range(1, 4):
        greet(seq, ((zl + d) % 4) * 2 + core, is_mid)

    def count(flag):
        return jnp.where(flag, 1, 0)

    expect = 3 + count(is_mid) + count(y < 7) + count((y >= 1) & (inner | (y >= 6)))
    expect = expect + count((y >= 5) & inner) + count(y <= 2) + count(row < 7) + count(row == 4)
    expect = expect + jnp.where(row == 0, 2, 0) + jnp.where(first, 7, 0)
    with jax.named_scope("greet"):
        pl.semaphore_wait(barrier, expect)

    for copy in kv_in:
        copy.wait()

    def own_hop(part):
        return remote(kv.at[0, part], kv.at[1, part], y_send.at[0, part], kv_recv.at[1, part], seq + 1, head)

    def far_hop(source, column, part):
        slot = jnp.where(column == 7, 7 - y, 8 - y)
        return remote(kv.at[source, part], kv.at[slot, part], far_send.at[part], kv_recv.at[slot, part],
                      row * 8 + column, head)

    def x_hop(part):
        return remote(kv.at[0, part], kv.at[8, part], x_send.at[part], kv_recv.at[8, part],
                      jnp.where(row == 3, seq - 24, seq + 8), head)

    crossing = row == 0

    def relay_of(slot):
        own = jnp.where((slot <= 3) & (y <= 6), 1, jnp.where(slot >= 6, -1, 0))
        before = jnp.where((slot >= 5) & (y >= 1), -1, jnp.where(slot <= 2, 1, 0))
        return jnp.where(slot <= y, own, before)

    def relay_hop(slot, part):
        turn = relay_of(slot)
        across = crossing & (slot == 8)
        to = jnp.where(across, seq + 32, row * 8 + (y + turn + 8) % 8)
        land = jnp.where(across, 8, slot + turn)
        return remote(kv.at[slot, part], kv.at[land, part], y_send.at[slot, part], kv_recv.at[land, part],
                      to, head)

    def held(slot):
        return (slot <= y) | inner | (slot == 8)

    def relays(slot):
        return (relay_of(slot) != 0) | (crossing & (slot == 8))

    sink_src = kv.at[0, 0, pl.ds(0, SINK_PAD), :]
    sink_src_v = kv.at[0, half, pl.ds(0, SINK_PAD), :]

    def sink_hops(keys, values, n, to):
        return [
            remote(keys, sink.at[0], s_send.at[n, 0], s_recv.at[0], to, head),
            remote(values, sink.at[1], s_send.at[n, 1], s_recv.at[1], to, head),
        ]

    forwards = (
        (0, 8, (row == 0) | (row == 1) | (row == 4) | (row == 5)),
        (1, 24, (row == 0) | (row == 4)),
        (2, 32, row == 0),
    )

    def pass_sinks(keys, values):
        for n, offset, flag in forwards:
            @pl.when(flag)
            def _(n=n, offset=offset):
                for copy in sink_hops(keys, values, n, seq + offset):
                    copy.start()

    @pl.when(first)
    def _():
        for d in range(1, 8):
            for copy in sink_hops(sink_src, sink_src_v, 2 + d, d):
                copy.start()
        pass_sinks(sink_src, sink_src_v)

    @pl.when(row < 7)
    def _():
        for part in range(PARTS):
            x_hop(part).start()

    @pl.when(y < 7)
    def _():
        for part in range(PARTS):
            own_hop(part).start()

    @pl.when(y <= 2)
    def _():
        for part in range(PARTS):
            far_hop(0, 7, part).start()

    w_hop = remote(w_ref, w_oth, w_send, w_recv, seq, partner)
    w_hop.start()

    for copy in later_in:
        copy.wait()
    q_f[...] = q_in[...].astype(F32)
    for p in range(2):
        for h in range(HEADS):
            for d in range(4):
                q_f2[pl.ds(p * HALF + h * 96 + d * OUT_TOK, OUT_TOK), :] = q_f[
                    pl.ds((2 * d + p) * OUT_TOK * HEADS + h, OUT_TOK, HEADS), :]
    qs[...] = q_f2[...].astype(BF)

    m_st[...] = jnp.full_like(m_st, NEG)
    l_st[...] = jnp.zeros_like(l_st)
    acc[...] = jnp.zeros_like(acc)
    scale2 = LOG2E / HD ** 0.5

    def column_facts(tile):
        col = tile * LANES + lax.broadcasted_iota(jnp.int32, (1, LANES), 1)
        p = col // HALF
        h = (col % HALF) // 96
        token = (2 * ((col % 96) // OUT_TOK) + p) * OUT_TOK + col % OUT_TOK

        def per_head(ref):
            value = jnp.where(h == 0, ref[0], ref[1])
            value = jnp.where(h == 2, ref[2], value)
            return jnp.where(h == 3, ref[3], value)

        return seq * TOK + token, per_head

    def fold(tile, scores, values):
        lanes = pl.ds(tile * LANES, LANES)
        m_old = m_st[:, lanes]
        m_new = jnp.maximum(m_old, jnp.max(scores, axis=0, keepdims=True))
        weights = jnp.exp2(scores - m_new)
        alpha = jnp.exp2(m_old - m_new)
        m_st[:, lanes] = m_new
        l_st[:, lanes] = l_st[:, lanes] * alpha + jnp.sum(weights, axis=0, keepdims=True)
        mixed = lax.dot_general(values, weights.astype(BF), (((0,), (0,)), ((), ())),
                                preferred_element_type=F32)
        acc[:, lanes] = acc[:, lanes] * alpha + mixed

    def score_tile(tile, keys):
        return lax.dot_general(keys, qs[pl.ds(tile * LANES, LANES), :], (((1,), (1,)), ((), ())),
                               preferred_element_type=F32) * scale2

    def attend(slot):
        keys = kv[slot, :half].reshape(TOK, HD)
        values = kv[slot, half:].reshape(TOK, HD)
        for tile in range(ROWS // LANES):
            pos, per_head = column_facts(tile)
            key_pos = (seq - slot) * TOK + lax.broadcasted_iota(jnp.int32, (TOK, LANES), 0)
            distance = pos - key_pos
            visible = (distance >= 0) & (distance < per_head(win_ref)) & (key_pos >= per_head(cnt_ref))
            fold(tile, jnp.where(visible, score_tile(tile, keys), NEG), values)

    def attend_sinks():
        keys, values = sink[0], sink[1]
        for tile in range(ROWS // LANES):
            pos, per_head = column_facts(tile)
            key_pos = lax.broadcasted_iota(jnp.int32, (SINK_PAD, LANES), 0)
            visible = (pos >= key_pos) & (key_pos < per_head(cnt_ref))
            scores = score_tile(tile, keys) + per_head(bias_ref) * LOG2E
            fold(tile, jnp.where(visible, scores, NEG), values)

    @pl.when(first)
    def _():
        sink[0] = kv[0, 0, :SINK_PAD, :]
        sink[1] = kv[0, half, :SINK_PAD, :]

    def sink_arrival():
        with jax.named_scope("sink_wait"):
            for copy in sink_hops(sink.at[0], sink.at[1], 0, seq):
                copy.wait_recv()

    def kv_arrival(slot, part):
        return remote(kv.at[slot, part], kv.at[slot, part], far_send.at[part], kv_recv.at[slot, part],
                      seq, partner)

    word = jnp.int32(0)
    for column in range(8):
        chosen = jnp.where(row == 4, packed(CROSSED[column]), packed(USUAL[column]))
        chosen = jnp.where(row == 0, packed(TOP[column]), chosen)
        word = jnp.where(y == column, chosen, word)
    sink_step = jnp.where(row == 0, 1, jnp.where(row == 5, 6, 4))
    passes = (row == 0) | (row == 1) | (row == 4) | (row == 5)

    with jax.named_scope("attend"):
        attend(0)

    def step(k, carry):
        slot = (lax.shift_right_logical(word, 3 * k) & 7) + 1

        @pl.when((k == sink_step) & passes & jnp.logical_not(first))
        def _():
            sink_arrival()
            pass_sinks(sink.at[0], sink.at[1])

        @pl.when(held(slot))
        def _():
            for part in range(PARTS):
                with jax.named_scope("kv_wait"):
                    kv_arrival(slot, part).wait_recv()

                @pl.when(relays(slot))
                def _(part=part):
                    relay_hop(slot, part).start()

                @pl.when((slot == 8) & (y >= 5) & inner)
                def _(part=part):
                    far_hop(8, 0, part).start()

        @pl.when(seq >= slot)
        def _():
            with jax.named_scope("attend"):
                attend(slot)

        return carry

    lax.fori_loop(0, 8, step, 0)

    @pl.when(jnp.logical_not(passes))
    def _():
        sink_arrival()

    attend_sinks()

    for tile in range(ROWS // 128):
        lanes = pl.ds(tile * 128, 128)
        done = acc[:, lanes] / l_st[:, lanes]
        a_buf[lanes, :] = done.T.astype(BF)

    mine = pl.multiple_of(core * HALF, HALF)
    theirs = pl.multiple_of(HALF - core * HALF, HALF)
    a_hop = remote(a_buf.at[pl.ds(theirs, HALF), :], a_oth, a_send, a_recv, seq, partner)
    a_hop.start()

    a_mine = jnp.concatenate(
        [a_buf[pl.ds(pl.multiple_of(mine + h * 96, 96), 96), :] for h in range(HEADS)], axis=1)
    w_copy.wait()

    for j in range(NC):
        cols = pl.ds(j * CN, CN)
        pacc[:, cols] = jnp.dot(a_mine, w_own[:, cols], preferred_element_type=F32)
    with jax.named_scope('a_wait'):
        a_hop.wait_recv()
    with jax.named_scope('w_wait'):
        w_hop.wait_recv()
    a_other = jnp.concatenate([a_oth[pl.ds(h * 96, 96), :] for h in range(HEADS)], axis=1)

    def item(d, j):
        return pacc[pl.ds(pl.multiple_of(d * OUT_TOK, 8), OUT_TOK), pl.ds(j * CN, CN)]

    def z_hop(n, j, to):
        return remote(sbuf.at[n, j], rbuf.at[zl, j], z_send.at[n, j], z_recv.at[zl, j], seq, to * 2 + core)

    def line_hop(j):
        return remote(sbuf.at[2, j], relay.at[j], z_send.at[2, j], relay_recv.at[j], seq, n1 * 2 + core)

    def relay_arrival(j):
        return remote(relay.at[j], relay.at[j], z_send.at[2, j], relay_recv.at[j], seq, partner)

    def z_arrival(source, j):
        return remote(rbuf.at[source, j], rbuf.at[source, j], z_send.at[0, j], z_recv.at[source, j], seq, partner)

    for j in range(NC):
        cols = pl.ds(j * CN, CN)
        pacc[:, cols] += jnp.dot(a_other, w_oth[:, cols], preferred_element_type=F32)

        @pl.when(is_end)
        def _(j=j):
            sbuf[2, j] = item(n3, j).astype(BF)
            line_hop(j).start()

        @pl.when(is_mid)
        def _(j=j):
            sbuf[0, j] = item(m2, j).astype(BF)
            z_hop(0, j, m2).start()
            sbuf[1, j] = item(e1, j).astype(BF)
            z_hop(1, j, e1).start()

    @pl.when(is_end)
    def _():
        for n, to in ((0, n2), (1, n1)):
            for j in range(NC):
                sbuf[n, j] = item(to, j).astype(BF)
                z_hop(n, j, to).start()

    @pl.when(is_mid)
    def _():
        for j in range(NC):
            with jax.named_scope('relay_wait'):
                relay_arrival(j).wait_recv()
            sbuf[2, j] = (item(e2, j) + relay[j].astype(F32)).astype(BF)
            z_hop(2, j, e2).start()

    def collect(sources):
        for j in range(NC):
            total = item(zl, j)
            for source in sources:
                with jax.named_scope('z_wait'):
                    z_arrival(source, j).wait_recv()
                total = total + rbuf[source, j].astype(F32)
            o_ref[:, pl.ds(j * CN, CN)] = total.astype(BF)

    @pl.when(is_end)
    def _():
        collect((n1, n2))

    @pl.when(is_mid)
    def _():
        collect((m2, e1, e2))

    @pl.when(row < 7)
    def _():
        for part in range(PARTS):
            x_hop(part).wait_send()

    @pl.when(y < 7)
    def _():
        for part in range(PARTS):
            own_hop(part).wait_send()

    @pl.when((y <= 2) | ((y >= 5) & inner))
    def _():
        for part in range(PARTS):
            far_hop(0, 7, part).wait_send()

    def drain(slot, carry):
        @pl.when(held(slot) & relays(slot))
        def _():
            for part in range(PARTS):
                relay_hop(slot, part).wait_send()

        return carry

    lax.fori_loop(1, 9, drain, 0)

    for n, offset, flag in forwards:
        @pl.when(flag)
        def _(n=n, offset=offset):
            for copy in sink_hops(sink.at[0], sink.at[1], n, seq + offset):
                copy.wait_send()

    @pl.when(first)
    def _():
        for d in range(1, 8):
            for copy in sink_hops(sink.at[0], sink.at[1], 2 + d, d):
                copy.wait_send()

    w_hop.wait_send()
    a_hop.wait_send()
    for j in range(NC):
        for n in range(3):
            z_hop(n, j, zl).wait_send()


def shards(queries, key_rows, value_rows, windows, sink_counts, sink_bias, out_weight):
    hbm = pl.BlockSpec(memory_space=pltpu.HBM)
    return pl.pallas_call(
        kernel,
        out_shape=pltpu.VMEM((OUT_TOK, D), BF),
        in_specs=[hbm] * 7,
        out_specs=pl.BlockSpec(memory_space=pltpu.VMEM),
        scratch_shapes=[
            pltpu.SMEM((HEADS,), jnp.int32),
            pltpu.SMEM((HEADS,), jnp.int32),
            pltpu.SMEM((HEADS,), F32),
            pltpu.VMEM((9, PARTS, PART_ROWS, HD), BF),
            pltpu.VMEM((2, SINK_PAD, HD), BF),
            pltpu.VMEM((ROWS, HD), BF),
            pltpu.VMEM((ROWS, HD), F32),
            pltpu.VMEM((ROWS, HD), F32),
            pltpu.VMEM((ROWS, HD), BF),
            pltpu.VMEM((KW, D), BF),
            pltpu.VMEM((KW, D), BF),
            pltpu.VMEM((HD, ROWS), F32),
            pltpu.VMEM((1, ROWS), F32),
            pltpu.VMEM((1, ROWS), F32),
            pltpu.VMEM((ROWS, HD), BF),
            pltpu.VMEM((HALF, HD), BF),
            pltpu.VMEM((96, D), F32),
            pltpu.VMEM((3, NC, OUT_TOK, CN), BF),
            pltpu.VMEM((4, NC, OUT_TOK, CN), BF),
            pltpu.VMEM((NC, OUT_TOK, CN), BF),
            pltpu.SemaphoreType.DMA((PARTS + 5,)),
            pltpu.SemaphoreType.DMA((PARTS,)),
            pltpu.SemaphoreType.DMA((9, PARTS)),
            pltpu.SemaphoreType.DMA((PARTS,)),
            pltpu.SemaphoreType.DMA((9, PARTS)),
            pltpu.SemaphoreType.DMA((10, 2)),
            pltpu.SemaphoreType.DMA((2,)),
            pltpu.SemaphoreType.DMA,
            pltpu.SemaphoreType.DMA,
            pltpu.SemaphoreType.DMA,
            pltpu.SemaphoreType.DMA,
            pltpu.SemaphoreType.DMA((3, NC)),
            pltpu.SemaphoreType.DMA((4, NC)),
            pltpu.SemaphoreType.DMA((NC,)),
        ],
        compiler_params=pltpu.CompilerParams(
            collective_id=0, has_side_effects=True, vmem_limit_bytes=67043328 - 512 * 1024),
    )(windows, sink_counts, sink_bias, queries.reshape(ROWS, HD), key_rows.reshape(TOK, HD),
      value_rows.reshape(TOK, HD), out_weight)


def solution(mesh):
    return jax.shard_map(
        shards,
        mesh=mesh,
        in_specs=(
            P("seq", "head", None),
            P("seq", "head", None),
            P("seq", "head", None),
            P("head"),
            P("head"),
            P("head"),
            P("head", None),
        ),
        out_specs=P(("seq", "head"), None),
        check_vma=False,
    )
```

time: 67.6 us -> 51 us (0.75)
  the two profiles are of different devices: /device:TPU:257 before, /device:TPU:3 now
where the time goes in v2:
time: 51 us; the launch traced here: 50.9 us
  Pallas kernels  50.2 us (98%)
  local copies, waits for them, and re-layouts  0.68 us (1%)
    pallas_call x1, Pallas kernels, shards(): pl.pallas_call(kernel, out_shape=pltpu.VMEM((OUT_TOK, D), BF), in_specs=[...  50.2 us

profile of v2, /device:TPU:3, one launch (start us, length us, event | category | flops | bytes accessed | tf_op | source)
XLA Modules:
  0.0 50.9 jit_solution(12986041984936334663)
XLA Ops:
  0.0 50.2 %shard_map.73 = bf16[24,4096]{1,0:T(8,128)(2,1)S(1)} custom-call(s32[4]{0:T(128)} %win_in.1, s32[4]{0:T(128)} %cnt_in.1, f32[4]{0:T(128)} %bias_in.1, bf16[768,128]{1,0:T(8,128)(2,1)} %bitcast.3, bf16[192,128]{1,0:T(8,128)(2,1)} %bitcast.4, bf16[192,128]{1,0:T(8,128)(2,1)} %bitcast.5, bf16[512,4096]{1,0:T(8,128)(2,1)} %w_ref.1), custom_call_target="tpu_custom_call" | custom-call | tf_op jit(solution)/shard_map/pallas_call | solution.py:487
  50.2 0.7 %copy.9 = bf16[24,4096]{1,0:T(8,128)(2,1)} copy(bf16[24,4096]{1,0:T(8,128)(2,1)S(1)} %shard_map.73) | data formatting | bytes 393216

commit v3 on v2

--- a/solution.py
+++ b/solution.py
@@ -27,14 +27,14 @@
 
 
 USUAL = (
-    (8, 1, 2, 7, 6, 5, 3, 4),
-    (1, 8, 7, 6, 2, 5, 3, 4),
-    (1, 8, 2, 7, 6, 5, 3, 4),
-    (1, 8, 2, 7, 3, 6, 5, 4),
-    (1, 8, 2, 7, 3, 6, 5, 4),
-    (1, 8, 7, 2, 6, 3, 5, 4),
-    (8, 7, 2, 6, 1, 5, 3, 4),
-    (8, 7, 6, 1, 3, 5, 2, 4),
+    (1, 2, 3, 8, 7, 6, 5, 4),
+    (8, 1, 7, 6, 5, 3, 2, 4),
+    (8, 7, 6, 3, 1, 2, 4, 5),
+    (8, 1, 2, 6, 5, 7, 4, 3),
+    (8, 1, 7, 2, 4, 6, 5, 3),
+    (8, 1, 7, 2, 6, 5, 3, 4),
+    (8, 7, 1, 6, 4, 2, 5, 3),
+    (8, 7, 1, 5, 6, 2, 3, 4),
 )
 CROSSED = (
     (8, 1, 7, 2, 6, 5, 3, 4),
@@ -47,19 +47,62 @@
     (1, 7, 8, 3, 6, 5, 2, 4),
 )
 TOP = (
-    (8, 1, 2, 3, 4, 5, 6, 7),
-    (8, 1, 2, 3, 4, 5, 6, 7),
-    (8, 1, 2, 3, 4, 5, 6, 7),
-    (8, 1, 2, 3, 4, 5, 6, 7),
-    (8, 1, 2, 3, 4, 5, 6, 7),
-    (8, 1, 2, 3, 5, 4, 6, 7),
-    (8, 1, 2, 6, 3, 5, 4, 7),
-    (8, 7, 1, 6, 3, 5, 2, 4),
+    (8, 1, 2, 3, 7, 6, 5, 4),
+    (8, 1, 7, 6, 5, 3, 2, 4),
+    (8, 1, 2, 7, 6, 3, 4, 5),
+    (8, 1, 2, 3, 6, 5, 7, 4),
+    (8, 1, 2, 4, 3, 7, 6, 5),
+    (8, 1, 2, 5, 3, 4, 7, 6),
+    (8, 1, 6, 4, 2, 5, 3, 7),
+    (8, 7, 1, 5, 6, 2, 3, 4),
 )
+USUAL_PASS = (
+    ((1, 7, 2), (2,), (1, 2), (1,), (), (), (), (), ()),
+    ((3, 7), (4,), (), (), (), (0,), (0,), (0,), (0,)),
+    ((3, 7), (), (), (3, 1), (), (), (1,), (1,), (1,)),
+    ((4,), (4,), (5, 2, 4), (), (), (), (2,), (), (2,)),
+    ((5, 6), (5,), (5,), (), (3,), (), (), (3,), (3, 2)),
+    ((6,), (7,), (7, 6), (), (), (), (4,), (3, 4), (4, 0)),
+    ((7,), (7,), (), (), (), (), (), (5,), (0, 5)),
+    ((), (), (), (), (), (6,), (6,), (5, 6), (6, 0)),
+)
+CROSSED_PASS = (
+    ((1, 7), (1,), (1,), (), (), (), (), (), ()),
+    ((2, 7), (2,), (2,), (), (), (0,), (0,), (0,), (0,)),
+    ((3, 7), (3,), (3,), (), (), (1,), (1,), (1,), (1,)),
+    ((4,), (4,), (4,), (4,), (), (2,), (2,), (2,), (2,)),
+    ((5,), (5,), (5,), (5,), (), (3,), (3,), (3,), (3,)),
+    ((6,), (6,), (6,), (6,), (), (), (4,), (4,), (4, 0)),
+    ((7,), (7,), (7,), (7,), (), (), (5,), (5,), (5, 0)),
+    ((), (), (), (), (), (), (6,), (6,), (6, 0)),
+)
+FAN = 3
 
 
 def packed(order):
     return sum((slot - 1) << (3 * k) for k, slot in enumerate(order))
+
+
+def pass_word(table, y, i):
+    word = 0
+    for slot, columns in enumerate(table[y]):
+        if i < len(columns):
+            word |= ((columns[i] - y) % 8) << (3 * slot)
+    return word
+
+
+def peer_word(table, y, own_only):
+    senders, receivers = set(), set()
+    for column in range(8):
+        for slot, columns in enumerate(table[column]):
+            if own_only and slot > column:
+                continue
+            if column == y:
+                receivers.update(columns)
+            if y in columns:
+                senders.add(column)
+    mask = sum(1 << ((column - y) % 8) for column in senders)
+    return mask + 256 * len(receivers)
 
 
 def remote(src, dst, send, recv, seq, head):
@@ -72,8 +115,8 @@
 def kernel(win_in, cnt_in, bias_in, q_ref, k_ref, v_ref, w_ref, o_ref,
            win_ref, cnt_ref, bias_ref, kv, sink, q_in, q_f, q_f2, qs, w_own, w_oth, acc, m_st, l_st, a_buf, a_oth, pacc,
            sbuf, rbuf, relay,
-           in_sem, x_send, y_send, far_send, kv_recv, s_send, s_recv, w_send, w_recv, a_send, a_recv,
-           z_send, z_recv, relay_recv):
+           in_sem, x_send, y_send, kv_recv, s_send, s_recv, w_send, w_recv, a_send, a_recv,
+           z_send, z_recv, relay_recv, ready):
     seq = lax.axis_index("seq")
     head = lax.axis_index("head")
     row, y = seq // 8, seq % 8
@@ -98,6 +141,17 @@
         copy.start()
     w_copy.start()
 
+    def choose(top, crossed, usual):
+        word = jnp.int32(0)
+        for column in range(8):
+            chosen = jnp.where(row == 4, crossed(column), usual(column))
+            chosen = jnp.where(row == 0, top(column), chosen)
+            word = jnp.where(y == column, chosen, word)
+        return word
+
+    peers = choose(lambda c: peer_word(USUAL_PASS, c, True), lambda c: peer_word(CROSSED_PASS, c, False),
+                   lambda c: peer_word(USUAL_PASS, c, False))
+
     is_end = (zl == 0) | (zl == 3)
     is_mid = jnp.logical_not(is_end)
     n1 = 1 + zl // 3
@@ -120,14 +174,12 @@
         else:
             pl.when(when)(signal)
 
-    greet(seq - 1, head, y >= 1)
-    greet(seq + 1, head, (y <= 6) & (inner | (y >= 5)))
-    for d in (5, 6, 7):
-        greet(seq + d, head, (y == 0) & inner)
-    for d in (7, 6, 5):
-        greet(seq - d, head, y == 7)
-    greet(jnp.where(row == 0, seq + 24, jnp.where(row == 4, seq - 32, seq - 8)), head)
+    for turn in range(1, 8):
+        greet(row * 8 + (y + turn) % 8, head, (lax.shift_right_logical(peers, turn) & 1) == 1)
+    greet(jnp.where(row == 0, seq + 24, seq - 8), head, row != 4)
+    greet(seq + 32, head, row == 0)
     greet(seq - 24, head, (row == 3) | (row == 7))
+    greet(seq - 16, head, (row == 2) | (row == 6))
     greet(row * 8, head, (row == 0) & (y >= 1))
     greet(seq, partner)
     greet(seq, n1 * 2 + core, is_end)
@@ -138,47 +190,49 @@
     def count(flag):
         return jnp.where(flag, 1, 0)
 
-    expect = 3 + count(is_mid) + count(y < 7) + count((y >= 1) & (inner | (y >= 6)))
-    expect = expect + count((y >= 5) & inner) + count(y <= 2) + count(row < 7) + count(row == 4)
-    expect = expect + jnp.where(row == 0, 2, 0) + jnp.where(first, 7, 0)
+    expect = 3 + count(is_mid) + lax.shift_right_logical(peers, 8) + count(row < 7)
+    expect = expect + jnp.where(row == 0, 2, 0) + jnp.where(row == 4, 3, 0) + jnp.where(first, 7, 0)
     with jax.named_scope("greet"):
         pl.semaphore_wait(barrier, expect)
 
+    @pl.when(row == 4)
+    def _():
+        pl.semaphore_signal(ready, inc=1, device_id=(seq - 32, head), device_id_type=MESH)
+
+    passed = [
+        choose(lambda c, i=i: pass_word(USUAL_PASS, c, i), lambda c, i=i: pass_word(CROSSED_PASS, c, i),
+               lambda c, i=i: pass_word(USUAL_PASS, c, i))
+        for i in range(FAN)
+    ]
+    word = choose(lambda c: packed(TOP[c]), lambda c: packed(CROSSED[c]), lambda c: packed(USUAL[c]))
+
     for copy in kv_in:
         copy.wait()
-
-    def own_hop(part):
-        return remote(kv.at[0, part], kv.at[1, part], y_send.at[0, part], kv_recv.at[1, part], seq + 1, head)
-
-    def far_hop(source, column, part):
-        slot = jnp.where(column == 7, 7 - y, 8 - y)
-        return remote(kv.at[source, part], kv.at[slot, part], far_send.at[part], kv_recv.at[slot, part],
-                      row * 8 + column, head)
 
     def x_hop(part):
         return remote(kv.at[0, part], kv.at[8, part], x_send.at[part], kv_recv.at[8, part],
                       jnp.where(row == 3, seq - 24, seq + 8), head)
 
     crossing = row == 0
-
-    def relay_of(slot):
-        own = jnp.where((slot <= 3) & (y <= 6), 1, jnp.where(slot >= 6, -1, 0))
-        before = jnp.where((slot >= 5) & (y >= 1), -1, jnp.where(slot <= 2, 1, 0))
-        return jnp.where(slot <= y, own, before)
-
-    def relay_hop(slot, part):
-        turn = relay_of(slot)
-        across = crossing & (slot == 8)
-        to = jnp.where(across, seq + 32, row * 8 + (y + turn + 8) % 8)
-        land = jnp.where(across, 8, slot + turn)
-        return remote(kv.at[slot, part], kv.at[land, part], y_send.at[slot, part], kv_recv.at[land, part],
-                      to, head)
+    passes = (row == 0) | (row == 4)
+
+    def turn_of(slot, i):
+        return lax.shift_right_logical(passed[i], 3 * slot) & 7
+
+    def relay_hop(slot, i, part):
+        column = (y + turn_of(slot, i)) % 8
+        land = slot + column - y
+        return remote(kv.at[slot, part], kv.at[land, part], y_send.at[slot, i, part], kv_recv.at[land, part],
+                      row * 8 + column, head)
+
+    def cross_hop(part):
+        return remote(kv.at[8, part], kv.at[8, part], y_send.at[8, 0, part], kv_recv.at[8, part], seq + 32, head)
 
     def held(slot):
         return (slot <= y) | inner | (slot == 8)
 
-    def relays(slot):
-        return (relay_of(slot) != 0) | (crossing & (slot == 8))
+    def relays(slot, i):
+        return (turn_of(slot, i) != 0) & ((slot <= y) | inner)
 
     sink_src = kv.at[0, 0, pl.ds(0, SINK_PAD), :]
     sink_src_v = kv.at[0, half, pl.ds(0, SINK_PAD), :]
@@ -190,13 +244,14 @@
         ]
 
     forwards = (
-        (0, 8, (row == 0) | (row == 1) | (row == 4) | (row == 5)),
-        (1, 24, (row == 0) | (row == 4)),
-        (2, 32, row == 0),
+        (0, 8, passes),
+        (1, 16, passes),
+        (2, 24, passes),
+        (3, 32, row == 0),
     )
 
-    def pass_sinks(keys, values):
-        for n, offset, flag in forwards:
+    def pass_sinks(keys, values, chosen):
+        for n, offset, flag in forwards[chosen]:
             @pl.when(flag)
             def _(n=n, offset=offset):
                 for copy in sink_hops(keys, values, n, seq + offset):
@@ -205,24 +260,20 @@
     @pl.when(first)
     def _():
         for d in range(1, 8):
-            for copy in sink_hops(sink_src, sink_src_v, 2 + d, d):
+            for copy in sink_hops(sink_src, sink_src_v, 3 + d, d):
                 copy.start()
-        pass_sinks(sink_src, sink_src_v)
+        pass_sinks(sink_src, sink_src_v, slice(0, 3))
 
     @pl.when(row < 7)
     def _():
         for part in range(PARTS):
             x_hop(part).start()
 
-    @pl.when(y < 7)
-    def _():
-        for part in range(PARTS):
-            own_hop(part).start()
-
-    @pl.when(y <= 2)
-    def _():
-        for part in range(PARTS):
-            far_hop(0, 7, part).start()
+    for i in range(FAN):
+        @pl.when(relays(0, i))
+        def _(i=i):
+            for part in range(PARTS):
+                relay_hop(0, i, part).start()
 
     w_hop = remote(w_ref, w_oth, w_send, w_recv, seq, partner)
     w_hop.start()
@@ -301,16 +352,10 @@
                 copy.wait_recv()
 
     def kv_arrival(slot, part):
-        return remote(kv.at[slot, part], kv.at[slot, part], far_send.at[part], kv_recv.at[slot, part],
+        return remote(kv.at[slot, part], kv.at[slot, part], x_send.at[part], kv_recv.at[slot, part],
                       seq, partner)
 
-    word = jnp.int32(0)
-    for column in range(8):
-        chosen = jnp.where(row == 4, packed(CROSSED[column]), packed(USUAL[column]))
-        chosen = jnp.where(row == 0, packed(TOP[column]), chosen)
-        word = jnp.where(y == column, chosen, word)
-    sink_step = jnp.where(row == 0, 1, jnp.where(row == 5, 6, 4))
-    passes = (row == 0) | (row == 1) | (row == 4) | (row == 5)
+    sink_step = jnp.where((row == 0) | (y == 0), 1, 3)
 
     with jax.named_scope("attend"):
         attend(0)
@@ -321,7 +366,21 @@
         @pl.when((k == sink_step) & passes & jnp.logical_not(first))
         def _():
             sink_arrival()
-            pass_sinks(sink.at[0], sink.at[1])
+            pass_sinks(sink.at[0], sink.at[1], slice(0, 4))
+
+        @pl.when((k == sink_step) & first)
+        def _():
+            pass_sinks(sink_src, sink_src_v, slice(3, 4))
+
+        @pl.when(k == 7)
+        def _():
+            @pl.when(jnp.logical_not(passes))
+            def _():
+                sink_arrival()
+
+            attend_sinks()
+
+        across = crossing & (slot == 8)
 
         @pl.when(held(slot))
         def _():
@@ -329,13 +388,16 @@
                 with jax.named_scope("kv_wait"):
                     kv_arrival(slot, part).wait_recv()
 
-                @pl.when(relays(slot))
+                @pl.when(across)
                 def _(part=part):
-                    relay_hop(slot, part).start()
-
-                @pl.when((slot == 8) & (y >= 5) & inner)
-                def _(part=part):
-                    far_hop(8, 0, part).start()
+                    if part == 0:
+                        pl.semaphore_wait(ready, 1)
+                    cross_hop(part).start()
+
+                for i in range(FAN):
+                    @pl.when(relays(slot, i))
+                    def _(part=part, i=i):
+                        relay_hop(slot, i, part).start()
 
         @pl.when(seq >= slot)
         def _():
@@ -346,11 +408,6 @@
 
     lax.fori_loop(0, 8, step, 0)
 
-    @pl.when(jnp.logical_not(passes))
-    def _():
-        sink_arrival()
-
-    attend_sinks()
 
     for tile in range(ROWS // 128):
         lanes = pl.ds(tile * 128, 128)
@@ -381,11 +438,11 @@
     def z_hop(n, j, to):
         return remote(sbuf.at[n, j], rbuf.at[zl, j], z_send.at[n, j], z_recv.at[zl, j], seq, to * 2 + core)
 
-    def line_hop(j):
-        return remote(sbuf.at[2, j], relay.at[j], z_send.at[2, j], relay_recv.at[j], seq, n1 * 2 + core)
-
-    def relay_arrival(j):
-        return remote(relay.at[j], relay.at[j], z_send.at[2, j], relay_recv.at[j], seq, partner)
+    def line_hop(n, j):
+        return remote(sbuf.at[n, j], relay.at[n, j], z_send.at[n, j], relay_recv.at[n, j], seq, n1 * 2 + core)
+
+    def relay_arrival(n, j):
+        return remote(relay.at[n, j], relay.at[n, j], z_send.at[n, j], relay_recv.at[n, j], seq, partner)
 
     def z_arrival(source, j):
         return remote(rbuf.at[source, j], rbuf.at[source, j], z_send.at[0, j], z_recv.at[source, j], seq, partner)
@@ -396,30 +453,67 @@
 
         @pl.when(is_end)
         def _(j=j):
-            sbuf[2, j] = item(n3, j).astype(BF)
-            line_hop(j).start()
+            sbuf[0, j] = item(n3, j).astype(BF)
+            line_hop(0, j).start()
 
         @pl.when(is_mid)
         def _(j=j):
-            sbuf[0, j] = item(m2, j).astype(BF)
-            z_hop(0, j, m2).start()
-            sbuf[1, j] = item(e1, j).astype(BF)
-            z_hop(1, j, e1).start()
+            sbuf[2, j] = item(e1, j).astype(BF)
+            z_hop(2, j, e1).start()
 
     @pl.when(is_end)
     def _():
-        for n, to in ((0, n2), (1, n1)):
+        for j in range(NC):
+            sbuf[1, j] = item(n2, j).astype(BF)
+            line_hop(1, j).start()
+        for j in range(NC):
+            sbuf[2, j] = item(n1, j).astype(BF)
+            z_hop(2, j, n1).start()
+
+    @pl.when(row < 7)
+    def _():
+        for part in range(PARTS):
+            x_hop(part).wait_send()
+
+    def drain(slot, carry):
+        for i in range(FAN):
+            @pl.when(relays(slot, i))
+            def _(i=i):
+                for part in range(PARTS):
+                    relay_hop(slot, i, part).wait_send()
+
+        return carry
+
+    lax.fori_loop(0, 9, drain, 0)
+
+    @pl.when(crossing)
+    def _():
+        for part in range(PARTS):
+            cross_hop(part).wait_send()
+
+
+    for n, offset, flag in forwards:
+        @pl.when(flag)
+        def _(n=n, offset=offset):
+            for copy in sink_hops(sink.at[0], sink.at[1], n, seq + offset):
+                copy.wait_send()
+
+    @pl.when(first)
+    def _():
+        for d in range(1, 8):
+            for copy in sink_hops(sink.at[0], sink.at[1], 3 + d, d):
+                copy.wait_send()
+
+    w_hop.wait_send()
+    a_hop.wait_send()
+    @pl.when(is_mid)
+    def _():
+        for n, to in ((0, e2), (1, m2)):
             for j in range(NC):
-                sbuf[n, j] = item(to, j).astype(BF)
+                with jax.named_scope("relay_wait"):
+                    relay_arrival(n, j).wait_recv()
+                sbuf[n, j] = (item(to, j) + relay[n, j].astype(F32)).astype(BF)
                 z_hop(n, j, to).start()
-
-    @pl.when(is_mid)
-    def _():
-        for j in range(NC):
-            with jax.named_scope('relay_wait'):
-                relay_arrival(j).wait_recv()
-            sbuf[2, j] = (item(e2, j) + relay[j].astype(F32)).astype(BF)
-            z_hop(2, j, e2).start()
 
     def collect(sources):
         for j in range(NC):
@@ -436,47 +530,8 @@
 
     @pl.when(is_mid)
     def _():
-        collect((m2, e1, e2))
-
-    @pl.when(row < 7)
-    def _():
-        for part in range(PARTS):
-            x_hop(part).wait_send()
-
-    @pl.when(y < 7)
-    def _():
-        for part in range(PARTS):
-            own_hop(part).wait_send()
-
-    @pl.when((y <= 2) | ((y >= 5) & inner))
-    def _():
-        for part in range(PARTS):
-            far_hop(0, 7, part).wait_send()
-
-    def drain(slot, carry):
-        @pl.when(held(slot) & relays(slot))
-        def _():
-            for part in range(PARTS):
-                relay_hop(slot, part).wait_send()
-
-        return carry
-
-    lax.fori_loop(1, 9, drain, 0)
-
-    for n, offset, flag in forwards:
-        @pl.when(flag)
-        def _(n=n, offset=offset):
-            for copy in sink_hops(sink.at[0], sink.at[1], n, seq + offset):
-                copy.wait_send()
-
-    @pl.when(first)
-    def _():
-        for d in range(1, 8):
-            for copy in sink_hops(sink.at[0], sink.at[1], 2 + d, d):
-                copy.wait_send()
-
-    w_hop.wait_send()
-    a_hop.wait_send()
+        collect((e1, m2))
+
     for j in range(NC):
         for n in range(3):
             z_hop(n, j, zl).wait_send()
@@ -509,13 +564,12 @@
             pltpu.VMEM((96, D), F32),
             pltpu.VMEM((3, NC, OUT_TOK, CN), BF),
             pltpu.VMEM((4, NC, OUT_TOK, CN), BF),
-            pltpu.VMEM((NC, OUT_TOK, CN), BF),
+            pltpu.VMEM((2, NC, OUT_TOK, CN), BF),
             pltpu.SemaphoreType.DMA((PARTS + 5,)),
             pltpu.SemaphoreType.DMA((PARTS,)),
+            pltpu.SemaphoreType.DMA((9, FAN, PARTS)),
             pltpu.SemaphoreType.DMA((9, PARTS)),
-            pltpu.SemaphoreType.DMA((PARTS,)),
-            pltpu.SemaphoreType.DMA((9, PARTS)),
-            pltpu.SemaphoreType.DMA((10, 2)),
+            pltpu.SemaphoreType.DMA((11, 2)),
             pltpu.SemaphoreType.DMA((2,)),
             pltpu.SemaphoreType.DMA,
             pltpu.SemaphoreType.DMA,
@@ -523,7 +577,8 @@
             pltpu.SemaphoreType.DMA,
             pltpu.SemaphoreType.DMA((3, NC)),
             pltpu.SemaphoreType.DMA((4, NC)),
-            pltpu.SemaphoreType.DMA((NC,)),
+            pltpu.SemaphoreType.DMA((2, NC)),
+            pltpu.SemaphoreType.REGULAR,
         ],
         compiler_params=pltpu.CompilerParams(
             collective_id=0, has_side_effects=True, vmem_limit_bytes=67043328 - 512 * 1024),

time: 51 us -> 48.9 us (0.959)
  the two profiles are of different devices: /device:TPU:3 before, /device:TPU:385 now
where the time goes in v3:
time: 48.9 us; the launch traced here: 48.7 us
  Pallas kernels  48.1 us (98%)
  local copies, waits for them, and re-layouts  0.68 us (1%)
    pallas_call x1, Pallas kernels, shards(): pl.pallas_call(kernel, out_shape=pltpu.VMEM((OUT_TOK, D), BF), in_specs=[...  48.1 us

profile of v3, /device:TPU:385, one launch (start us, length us, event | category | flops | bytes accessed | tf_op | source)
XLA Modules:
  0.0 48.7 jit_solution(17451165898301546097)
XLA Ops:
  0.0 48.1 %shard_map.73 = bf16[24,4096]{1,0:T(8,128)(2,1)S(1)} custom-call(s32[4]{0:T(128)} %win_in.1, s32[4]{0:T(128)} %cnt_in.1, f32[4]{0:T(128)} %bias_in.1, bf16[768,128]{1,0:T(8,128)(2,1)} %bitcast.3, bf16[192,128]{1,0:T(8,128)(2,1)} %bitcast.4, bf16[192,128]{1,0:T(8,128)(2,1)} %bitcast.5, bf16[512,4096]{1,0:T(8,128)(2,1)} %w_ref.1), custom_call_target="tpu_custom_call" | custom-call | tf_op jit(solution)/shard_map/pallas_call | solution.py:542
  48.1 0.7 %copy.9 = bf16[24,4096]{1,0:T(8,128)(2,1)} copy(bf16[24,4096]{1,0:T(8,128)(2,1)S(1)} %shard_map.73) | data formatting | bytes 393216
